TPU v7x, 32 devices: a whole 2x2x4 slice. The times are simulated.
32 devices in a mesh: batch: 8 (over z, core), vocab: 4 (over y, x).
Axes of the slice: x: 2, y: 2, z: 4, core: 2. Of those that a mesh axis runs over, the one named last changes fastest.
Arguments:
- window_ids: int32 [3, 16, 8], P(None, 'batch'), may hold values from 0 to 16383
- pool_ids: int32 [3, 16, 8], P(None, 'batch'), may hold values from 0 to 16383
- accepted: int32 [2, 16], P(None, 'batch'), may hold values from 1 to 8
- converged: int32 [2, 16], P(None, 'batch'), may hold values 0 or 1
- cache_lens: int32 [16], P('batch'), may hold values from 1 to 128
- table: bfloat16 [16384, 4608], P(('batch', 'vocab')), may hold values from -0.29882812 to 0.29882812
- attn_gain: float32 [4608], replicated, may hold values from 0.25 to 1.75
- post_gain: float32 [4608], replicated, may hold values from 0.25 to 1.75
- final_gain: float32 [4608], replicated, may hold values from 0.25 to 1.75
- w_query: bfloat16 [4608, 1024], P(None, 'vocab'), may hold values from -0.09375 to 0.09375
- w_key: bfloat16 [4608, 512], P(None, 'vocab'), may hold values from -0.09375 to 0.09375
- w_value: bfloat16 [4608, 512], P(None, 'vocab'), may hold values from -0.09375 to 0.09375
- w_out: bfloat16 [1024, 4608], P('vocab'), may hold values from -0.1875 to 0.1875
- cache_keys: bfloat16 [16, 4, 128, 128], P('batch', 'vocab'), may hold values from -6 to 6
- cache_values: bfloat16 [16, 4, 128, 128], P('batch', 'vocab'), may hold values from -6 to 6
Outputs:
- log_total: float32 [3, 16, 8], P(None, 'batch')
- best_logit: float32 [3, 16, 8], P(None, 'batch')
- pool_score: float32 [3, 16, 8], P(None, 'batch')
Inputs may be any that keep to these rules, and one draw needn't show every extreme that they name: `converged`: 1 marks a window at its fixed point, whose tokens are all accepted.
All inputs are finite; a program needn't handle non-finite values. No bound on the sum of `converged` on one device may be relied on, other than what follows from the above.
Results may differ from a plain program's by a relative error of at most 0.00036.
Values may be sent and summed in bfloat16 or wider, within the bound.
No kernel may reach another device: no remote copies, remote signals or barrier semaphores. Data moves between devices by JAX's collectives and lax.ppermute only.
A program may use at most 128 MiB of HBM per device.

v0:
```python
import math
import jax
import jax.numpy as jnp
from jax import lax
from jax.sharding import PartitionSpec as P

epsilon = 1e-06
query_scalar = 144.0
score_cap = 50.0
logit_cap = 30.0


def normalize(values_in, gain):
    return (
        values_in
        * lax.rsqrt(jnp.mean(values_in * values_in, axis=-1, keepdims=True) + epsilon)
        * gain
    )


def rotate(values_in, positions):
    half_size = values_in.shape[-1] // 2
    freqs = 10000.0 ** (-jnp.arange(half_size, dtype=jnp.float32) / half_size)
    angles = positions.astype(jnp.float32)[..., None] * freqs
    cosine = jnp.cos(angles)
    sine = jnp.sin(angles)
    first_half = values_in[..., :half_size]
    second_half = values_in[..., half_size:]
    return jnp.concatenate(
        [first_half * cosine - second_half * sine, second_half * cosine + first_half * sine],
        axis=-1,
    )


def attend(queries, key_rows, value_rows, visible):
    scores = jnp.einsum("bwhgd,bhld->bhgwl", queries, key_rows, preferred_element_type=jnp.float32)
    scores = score_cap * jnp.tanh(scores / score_cap)
    weights = jnp.where(visible[:, None, None], jnp.exp(scores), 0.0)
    weight_sum = jnp.sum(weights, axis=-1, keepdims=True)
    rounded = lax.optimization_barrier(weights.astype(jnp.bfloat16))
    summed = jnp.einsum(
        "bhgwl,bhld->bwhgd", rounded, value_rows, preferred_element_type=jnp.float32
    )
    return (summed / jnp.moveaxis(weight_sum, 3, 1)).astype(jnp.bfloat16)


def per_device(
    window_ids,
    pool_ids,
    accepted,
    converged,
    cache_lens,
    table,
    attn_gain,
    post_gain,
    final_gain,
    w_query,
    w_key,
    w_value,
    w_out,
    cache_keys,
    cache_values,
):
    iter_count, local_batch, width = window_ids.shape
    model_width = table.shape[1]
    vocab_rows = table.shape[0]
    head_size = cache_keys.shape[3]
    kv_local = cache_keys.shape[1]
    cache_slots = cache_keys.shape[2]
    local_rows = local_batch * width
    vocab_devices = lax.axis_size("vocab")
    batch_index = lax.axis_index("batch")
    vocab_index = lax.axis_index("vocab")
    all_windows, all_pools = (
        lax.all_gather(window_ids, "batch", axis=1, tiled=True),
        lax.all_gather(pool_ids, "batch", axis=1, tiled=True),
    )
    total_batch = all_windows.shape[1]
    first_id = (batch_index * vocab_devices + vocab_index) * vocab_rows
    ordered = jnp.transpose(all_windows, (1, 2, 0)) - first_id
    inside = (ordered >= 0) & (ordered < vocab_rows)
    looked_up = jnp.take(table, jnp.clip(ordered, 0, vocab_rows - 1), axis=0)
    lookup_terms = jnp.where(inside[..., None], looked_up.astype(jnp.float32), 0.0)
    column_rows = lax.psum_scatter(
        lookup_terms.astype(jnp.bfloat16), "batch", scatter_dimension=0, tiled=True
    )
    embedded_all = lax.psum(column_rows, "vocab").astype(jnp.float32)
    taken = jnp.where(converged == 1, width, accepted)
    offset = cache_lens
    slots = jnp.arange(width, dtype=jnp.int32)
    cache_visible = (
        jnp.arange(cache_slots, dtype=jnp.int32)[None, None, :] < cache_lens[:, None, None]
    )
    own_visible = slots[None, None, :] <= slots[None, :, None]
    key_list = [cache_keys]
    value_list = [cache_values]
    mask_list = [jnp.broadcast_to(cache_visible, (local_batch, width, cache_slots))]
    vocab_iota = jnp.arange(vocab_rows, dtype=jnp.int32)
    totals_out = []
    best_out = []
    score_out = []
    for step in range(iter_count):
        embedded = embedded_all[:, :, step] * math.sqrt(model_width)
        normed = (
            normalize(embedded, attn_gain).astype(jnp.bfloat16).reshape(local_rows, model_width)
        )
        positions = (offset[:, None] + slots[None, :])[:, :, None]
        queries = jnp.dot(normed, w_query, preferred_element_type=jnp.float32).reshape(
            local_batch, width, 2 * kv_local, head_size
        )
        queries = (
            (rotate(queries, positions) / math.sqrt(query_scalar))
            .astype(jnp.bfloat16)
            .reshape(local_batch, width, kv_local, 2, head_size)
        )
        keys_now = jnp.dot(normed, w_key, preferred_element_type=jnp.float32).reshape(
            local_batch, width, kv_local, head_size
        )
        keys_now = rotate(keys_now, positions).astype(jnp.bfloat16).transpose(0, 2, 1, 3)
        values_now = jnp.dot(normed, w_value, preferred_element_type=jnp.float32).reshape(
            local_batch, width, kv_local, head_size
        )
        values_now = values_now.astype(jnp.bfloat16).transpose(0, 2, 1, 3)
        all_keys = jnp.concatenate(key_list + [keys_now], axis=2)
        all_values = jnp.concatenate(value_list + [values_now], axis=2)
        visible = jnp.concatenate(
            mask_list + [jnp.broadcast_to(own_visible, (local_batch, width, width))], axis=2
        )
        attended = attend(queries, all_keys, all_values, visible).reshape(
            local_rows, 2 * kv_local * head_size
        )
        branch = jnp.dot(attended, w_out, preferred_element_type=jnp.float32)
        residual = embedded.reshape(local_rows, model_width)
        whole_branch = lax.psum(branch, "vocab")
        hidden = residual + normalize(whole_branch, post_gain)
        final_rows = normalize(hidden, final_gain).astype(jnp.bfloat16)
        pool_local = all_pools[step].reshape(total_batch * width) - first_id
        raw_logits = lax.dot_general(
            lax.all_gather(final_rows, "batch", axis=0, tiled=True),
            table,
            (((1,), (1,)), ((), ())),
            preferred_element_type=jnp.float32,
        )
        logits = logit_cap * jnp.tanh(raw_logits / logit_cap)
        exp_sums = jnp.sum(jnp.exp(logits), axis=-1)
        largest = jnp.max(logits, axis=-1)
        chosen = jnp.sum(
            jnp.where(vocab_iota[None, :] == pool_local[:, None], logits, 0.0), axis=-1
        )
        own_start = batch_index * local_rows
        sums_column, picks_column = (
            lax.psum_scatter(exp_sums, "batch", scatter_dimension=0, tiled=True),
            lax.psum_scatter(chosen, "batch", scatter_dimension=0, tiled=True),
        )
        sums_own, picks_own = lax.psum((sums_column, picks_column), "vocab")
        tops_joint = lax.pmax(largest, ("batch", "vocab"))
        tops_own = lax.dynamic_slice_in_dim(tops_joint, own_start, local_rows)
        log_sum = jnp.log(sums_own)
        totals_out.append(log_sum.reshape(local_batch, width))
        best_out.append(tops_own.reshape(local_batch, width))
        score_out.append((picks_own - log_sum).reshape(local_batch, width))
        if step + 1 < iter_count:
            key_list.append(keys_now)
            value_list.append(values_now)
            mask_list.append(
                jnp.broadcast_to(
                    slots[None, None, :] < taken[step][:, None, None], (local_batch, width, width)
                )
            )
            offset = offset + taken[step]
    return (jnp.stack(totals_out), jnp.stack(best_out), jnp.stack(score_out))


def solution(mesh):
    return jax.shard_map(
        per_device,
        mesh=mesh,
        in_specs=(
            P(None, "batch", None),
            P(None, "batch", None),
            P(None, "batch"),
            P(None, "batch"),
            P("batch"),
            P(("batch", "vocab"), None),
            P(),
            P(),
            P(),
            P(None, "vocab"),
            P(None, "vocab"),
            P(None, "vocab"),
            P("vocab", None),
            P("batch", "vocab", None, None),
            P("batch", "vocab", None, None),
        ),
        out_specs=(P(None, "batch", None), P(None, "batch", None), P(None, "batch", None)),
        check_vma=False,
    )
```

profile of v0, /device:TPU:10, one launch (start us, length us, event | category | flops | bytes accessed | tf_op | source)
XLA Modules:
  0.0 360.0 jit_solution(6029630634133774123)
XLA Ops:
  8.1 14.3 %all_gather.15 = s32[3,16,8]{2,0,1:T(4,128)S(1)} all-gather(s32[3,2,8]{2,0,1:T(4,128)S(1)} %copy.76), channel_id=1, replica_groups=mesh['batch'=8,'vocab'=4] {'batch'}, dimensions={1}, use_global_device_ids=true | all-gather | bytes 1728 | tf_op jit(solution)/shard_map/all_gather | solution.py:75
  22.8 12.2 %gather_fusion = bf16[384,4608]{1,0:T(8,128)(2,1)} fusion(bf16[512,4608]{1,0:T(8,128)(2,1)} %param.20, s32[1024]{0:T(1024)S(1)} %pad_clamp_fusion), kind=kCustom, calls=%fused_computation | custom fusion | bytes 7079424 | tf_op jit(solution)/shard_map/jit(_take)/gather | solution.py:82
  35.0 7.3 %reshape.718 = bf16[16,8,3,4608]{3,2,1,0:T(4,128)(2,1)} reshape(bf16[384,4608]{1,0:T(8,128)(2,1)} %gather_fusion) | data formatting | bytes 7077888 | tf_op jit(solution)/shard_map/jit(_take)/gather | solution.py:82
  42.4 6.3 %select_convert_fusion = bf16[16,8,3,4608]{3,1,2,0:T(8,128)(2,1)} fusion(bf16[16,8,3,4608]{3,2,1,0:T(4,128)(2,1)} %reshape.718, pred[16,8,3]{1,2,0:T(4,128)(4,1)S(1)} %copy.79, pred[16,8,3]{1,2,0:T(4,128)(4,1)S(1)} %copy.78), kind=kLoop, calls=%fused_computation.1 | loop fusion | flops 7077888 | bytes 7078656 | tf_op jit(solution)/shard_map/convert_element_type | solution.py:85
  48.8 4.3 %copy.102 = bf16[256,4608]{1,0:T(8,128)(2,1)} copy(bf16[256,4608]{0,1:T(8,128)(2,1)} %bitcast.314) | data formatting | bytes 4718592 | tf_op jit(solution)/shard_map/dot_general | solution.py:108
  53.7 36.1 %reduce-scatter.2.cloned.1.call-done = bf16[2,8,3,4608]{3,1,2,0:T(8,128)(2,1)} async-done(((bf16[16,8,3,4608]{3,1,2,0:T(8,128)(2,1)}), bf16[2,8,3,4608]{3,1,2,0:T(8,128)(2,1)}) %reduce-scatter.2.cloned.1.call-update) | async-done | bytes 442384 | tf_op jit(solution)/shard_map/reduce_scatter | solution.py:84
  89.8 1.8 copy.82
  92.1 47.6 %all-reduce.13.cloned.1.call-done = bf16[2,8,3,4608]{3,1,0,2:T(8,128)(2,1)} async-done(((bf16[2,8,3,4608]{3,1,0,2:T(8,128)(2,1)}), bf16[2,8,3,4608]{3,1,0,2:T(8,128)(2,1)}) %all-reduce.13.cloned.1.call-update) | async-done | bytes 442384 | tf_op jit(solution)/shard_map/psum | solution.py:87
  141.1 1.6 fusion.45
  142.7 1.7 fusion.48
  151.1 1.2 fusion.70
  152.4 1.2 fusion.69
  153.7 50.5 %all-reduce.15.cloned.1.call-done = (f32[16,4608]{1,0:T(8,128)}, f32[16,4608]{1,0:T(8,128)}, f32[16,4608]{1,0:T(8,128)}) async-done(((f32[16,4608]{1,0:T(8,128)}, f32[16,4608]{1,0:T(8,128)}, f32[16,4608]{1,0:T(8,128)}), (f32[16,4608]{1,0:T(8,128)}, f32[16,4608]{1,0:T(8,128)}, f32[16,4608]{1,0:T(8,128)})) %all-reduce.15.cloned.1.call-update) | async-done | bytes 884752 | tf_op jit(solution)/shard_map/psum | solution.py:134
  207.7 1.5 multiply_reduce_fusion.4
  211.5 14.2 %all_gather.19 = s32[3,16,8]{2,0,1:T(4,128)S(1)} all-gather(s32[3,2,8]{2,0,1:T(4,128)S(1)} %copy.92), channel_id=1, replica_groups=mesh['batch'=8,'vocab'=4] {'batch'}, dimensions={1}, use_global_device_ids=true | all-gather | bytes 1728 | tf_op jit(solution)/shard_map/all_gather | solution.py:76
  227.3 5.9 %all-gather.4.cloned.1.call-done = bf16[128,4608]{1,0:T(8,128)(2,1)} async-done(((bf16[16,4608]{1,0:T(8,128)(2,1)}), bf16[128,4608]{1,0:T(8,128)(2,1)}) %all-gather.4.cloned.1.call-update) | async-done | bytes 1179664 | tf_op jit(solution)/shard_map/all_gather | solution.py:139
  233.2 4.5 %select_reduce_fusion.2 = (f32[128]{0:T(128)S(1)}, f32[128]{0:T(128)S(1)}, f32[128]{0:T(128)S(1)}) fusion(s32[128]{0:T(128)S(1)} %sub.79, bf16[128,4608]{1,0:T(8,128)(2,1)} %all-gather.4.cloned.1.call-done, bf16[512,4608]{1,0:T(8,128)(2,1)} %param.20), kind=kOutput, calls=%fused_computation.103 | convolution fusion | flops 604438144 | bytes 5900288 | tf_op jit(solution)/shard_map/dot_general | solution.py:138
  237.7 19.4 %all-gather.6.cloned.1.call-done = bf16[128,4608]{1,0:T(8,128)(2,1)} async-done(((bf16[16,4608]{1,0:T(8,128)(2,1)}), bf16[128,4608]{1,0:T(8,128)(2,1)}) %all-gather.6.cloned.1.call-update) | async-done | bytes 1179664 | tf_op jit(solution)/shard_map/all_gather | solution.py:139
  257.1 4.5 %select_reduce_fusion.1 = (f32[128]{0:T(128)S(1)}, f32[128]{0:T(128)S(1)}, f32[128]{0:T(128)S(1)}) fusion(s32[128]{0:T(128)S(1)} %sub.82, bf16[128,4608]{1,0:T(8,128)(2,1)} %all-gather.6.cloned.1.call-done, bf16[512,4608]{1,0:T(8,128)(2,1)} %param.20), kind=kOutput, calls=%fused_computation.101 | convolution fusion | flops 604438144 | bytes 5900288 | tf_op jit(solution)/shard_map/dot_general | solution.py:138
  261.6 19.5 %all-gather.8.cloned.1.call-done = bf16[128,4608]{1,0:T(8,128)(2,1)} async-done(((bf16[16,4608]{1,0:T(8,128)(2,1)}), bf16[128,4608]{1,0:T(8,128)(2,1)}) %all-gather.8.cloned.1.call-update) | async-done | bytes 1179664 | tf_op jit(solution)/shard_map/all_gather | solution.py:139
  281.0 4.5 %select_reduce_fusion = (f32[128]{0:T(128)S(1)}, f32[128]{0:T(128)S(1)}, f32[128]{0:T(128)S(1)}) fusion(s32[128]{0:T(128)S(1)} %sub.85, bf16[128,4608]{1,0:T(8,128)(2,1)} %all-gather.8.cloned.1.call-done, bf16[512,4608]{1,0:T(8,128)(2,1)} %param.20), kind=kOutput, calls=%fused_computation.99 | convolution fusion | flops 604438144 | bytes 5900288 | tf_op jit(solution)/shard_map/dot_general | solution.py:138
  285.5 12.1 %all-reduce.7 = (f32[128]{0:T(128)S(1)}, f32[128]{0:T(128)S(1)}, f32[128]{0:T(128)S(1)}, f32[128]{0:T(128)S(1)}, f32[128]{0:T(128)S(1)}, /*index=5*/f32[128]{0:T(128)S(1)}) all-reduce(f32[128]{0:T(128)S(1)} %get-tuple-element.17, f32[128]{0:T(128)S(1)} %get-tuple-element.14, ...), channel_id=5, replica_groups=mesh['batch'=8,'vocab'=4] {'batch'}, use_global_device_ids=true, to_apply=%region_24.25.clone | all-reduce | flops 768 | bytes 6144
  298.1 8.0 %all-reduce.8 = (f32[16]{0:T(128)S(1)}, f32[16]{0:T(128)S(1)}, f32[16]{0:T(128)S(1)}, f32[16]{0:T(128)S(1)}, f32[16]{0:T(128)S(1)}, /*index=5*/f32[16]{0:T(128)S(1)}) all-reduce(f32[16]{0:T(128)S(1)} %dynamic-slice.5, f32[16]{0:T(128)S(1)} %dynamic-slice.3, f32[16]{0:T(128)S(1)} %dynamic-slice.1, ...), channel_id=1, replica_groups=mesh['batch'=8,'vocab'=4] {'vocab'}, use_global_device_ids=true, to_apply=%region_25.26 | all-reduce | flops 96 | bytes 768 | tf_op jit(solution)/shard_map/psum | solution.py:155
  306.4 44.3 %all-reduce.6 = (f32[128]{0:T(128)S(1)}, f32[128]{0:T(128)S(1)}, f32[128]{0:T(128)S(1)}) all-reduce(f32[128]{0:T(128)S(1)} %get-tuple-element.16, f32[128]{0:T(128)S(1)} %get-tuple-element.13, f32[128]{0:T(128)S(1)} %get-tuple-element.10), channel_id=1, replica_groups=mesh['batch'=8,'vocab'=4] {'batch','vocab'}, use_global_device_ids=true, to_apply=%region_31.32 | all-reduce | flops 384 | bytes 3072 | tf_op jit(solution)/shard_map/pmax | solution.py:156
  (131 shorter events, 20.4 us)
Async XLA Ops:
  7.2 142.7 %copy-start = (bf16[256,4608]{1,0:T(8,128)(2,1)S(1)}, bf16[256,4608]{1,0:T(8,128)(2,1)}, u32[]{:S(2)}) copy-start(bf16[256,4608]{1,0:T(8,128)(2,1)} %param.27) | copy-start | bytes 7077892
  7.2 82.6 %reduce-scatter.2.cloned.1.call-start = ((), (), s32[]{:S(2)}) async-start(), calls=%async_computation.1 | async-start | bytes 3981312 | tf_op jit(solution)/shard_map/reduce_scatter | solution.py:84
  48.7 90.9 %all-reduce.13.cloned.1.call-start = ((), (), s32[]{:S(2)}) async-start(), calls=%async_computation.2 | async-start | bytes 884736 | tf_op jit(solution)/shard_map/psum | solution.py:87
  48.8 4.4 %copy-start.14 = (s32[2]{0:T(128)S(1)}, s32[2]{0:T(128)}, u32[]{:S(2)}) copy-start(s32[2]{0:T(128)} %param.19) | copy-start | bytes 28
  48.8 4.5 %copy-start.12 = (s32[2,2]{1,0:T(2,128)S(1)}, s32[2,2]{1,0:T(2,128)}, u32[]{:S(2)}) copy-start(s32[2,2]{1,0:T(2,128)} %param.17) | copy-start | bytes 52
  48.8 4.5 %copy-start.13 = (s32[2,2]{1,0:T(2,128)S(1)}, s32[2,2]{1,0:T(2,128)}, u32[]{:S(2)}) copy-start(s32[2,2]{1,0:T(2,128)} %param.18) | copy-start | bytes 52
  53.2 87.9 %copy-start.4 = (f32[4608]{0:T(1024)S(1)}, f32[4608]{0:T(1024)}, u32[]{:S(2)}) copy-start(f32[4608]{0:T(1024)} %param.21) | copy-start | bytes 55300
  91.6 112.6 %all-reduce.15.cloned.1.call-start = ((), (), s32[]{:S(2)}) async-start(), calls=%async_computation.6 | async-start | bytes 1769472 | tf_op jit(solution)/shard_map/psum | solution.py:134
  139.7 4.7 %copy-start.3 = (bf16[4608,128]{1,0:T(8,128)(2,1)S(1)}, bf16[4608,128]{1,0:T(8,128)(2,1)}, u32[]{:S(2)}) copy-start(bf16[4608,128]{1,0:T(8,128)(2,1)} %param.26) | copy-start | bytes 3538948
  142.6 2.4 copy-start.2
  144.7 1.7 copy-start.1
  147.1 1.7 copy-start.15
  147.8 2.1 copy-start.8
  152.4 55.3 %copy-start.9 = (f32[4608]{0:T(1024)S(1)}, f32[4608]{0:T(1024)}, u32[]{:S(2)}) copy-start(f32[4608]{0:T(1024)} %param.22) | copy-start | bytes 55300
  153.6 55.6 %copy-start.10 = (f32[4608]{0:T(1024)S(1)}, f32[4608]{0:T(1024)}, u32[]{:S(2)}) copy-start(f32[4608]{0:T(1024)} %param.23) | copy-start | bytes 55300
  153.6 79.6 %all-gather.4.cloned.1.call-start = ((), (), s32[]{:S(2)}) async-start(), calls=%async_computation.3 | async-start | bytes 1327104 | tf_op jit(solution)/shard_map/all_gather | solution.py:139
  204.2 5.1 %copy-start.5 = (f32[16,4608]{1,0:T(8,128)S(1)}, f32[16,4608]{1,0:T(8,128)}, u32[]{:S(2)}) copy-start(f32[16,4608]{1,0:T(8,128)} %get-tuple-element.36) | copy-start | bytes 884740
  204.2 5.1 %copy-start.6 = (f32[16,4608]{1,0:T(8,128)S(1)}, f32[16,4608]{1,0:T(8,128)}, u32[]{:S(2)}) copy-start(f32[16,4608]{1,0:T(8,128)} %get-tuple-element.37) | copy-start | bytes 884740
  204.2 5.1 %copy-start.7 = (f32[16,4608]{1,0:T(8,128)S(1)}, f32[16,4608]{1,0:T(8,128)}, u32[]{:S(2)}) copy-start(f32[16,4608]{1,0:T(8,128)} %get-tuple-element.38) | copy-start | bytes 884740
  206.5 4.9 %copy-start.11 = (s32[3,2,8]{2,1,0:T(2,128)S(1)}, s32[3,2,8]{2,1,0:T(2,128)}, u32[]{:S(2)}) copy-start(s32[3,2,8]{2,1,0:T(2,128)} %param.16) | copy-start | bytes 580
  207.6 18.4 %copy-start.16 = (u32[32]{0:T(128)S(1)}, u32[32]{0:T(128)}, u32[]{:S(2)}) copy-start(u32[32]{0:T(128)} %constant.94) | copy-start | bytes 388
  210.3 46.8 %all-gather.6.cloned.1.call-start = ((), (), s32[]{:S(2)}) async-start(), calls=%async_computation.4 | async-start | bytes 1327104 | tf_op jit(solution)/shard_map/all_gather | solution.py:139
  210.9 70.2 %all-gather.8.cloned.1.call-start = ((), (), s32[]{:S(2)}) async-start(), calls=%async_computation.5 | async-start | bytes 1327104 | tf_op jit(solution)/shard_map/all_gather | solution.py:139
Sparse Core Ops, SparseCore 0:
  48.9 40.8 reduce-scatter.1
  92.8 46.8 all-reduce.12
  153.7 50.3 all-reduce.14
  210.4 22.7 all-gather.3
  234.7 22.3 all-gather.5
  258.6 22.4 all-gather.7
where the time goes:
time: 361 us; the launch traced here: 360 us
  waiting for transfers between devices  180 us (50%)
  blocking collectives  92.9 us (26%)
  local copies, waits for them, and re-layouts  30 us (8%)
  matrix products  24.9 us (7%)
  other arithmetic  16.6 us (5%)
  between operations  15.1 us (4%)
    psum x1, waiting for transfers between devices, per_device(): whole_branch = lax.psum(branch, 'vocab')  50.5 us
    psum x1, waiting for transfers between devices, per_device(): embedded_all = lax.psum(column_rows, 'vocab').astype(jnp.float32)  47.6 us
    all_gather x3, waiting for transfers between devices, per_device(): lax.all_gather(final_rows, 'batch', axis=0, tiled=True)  44.7 us
    pmax x1, blocking collectives, per_device(): tops_joint = lax.pmax(largest, ('batch', 'vocab'))  44.3 us
    reduce_scatter x1, waiting for transfers between devices, per_device(): lax.psum_scatter(lookup_terms.astype(jnp.bfloat16), 'batch', scatter_dime...  36.1 us
    gather x2, local copies, waits for them, and re-layouts, per_device(): looked_up = jnp.take(table, jnp.clip(ordered, 0, vocab_rows - 1), axis=0)  19.4 us
    all_gather x1, blocking collectives, per_device(): lax.all_gather(window_ids, 'batch', axis=1, tiled=True)  14.3 us
    all_gather x1, blocking collectives, per_device(): lax.all_gather(pool_ids, 'batch', axis=1, tiled=True)  14.2 us
  transfers between devices with their start and end apart: 6, of which 6 were waited for; matrix products, arithmetic and copies ran while one was open for 4% of the time, Pallas kernels for 0%

commit v1 on v0

--- a/solution.py
+++ b/solution.py
@@ -8,6 +8,10 @@
 query_scalar = 144.0
 score_cap = 50.0
 logit_cap = 30.0
+make_slabs = lambda x0, which_axis: jnp.concatenate(
+    lax.all_to_all(jnp.stack([x0 for _ in range(lax.axis_size(which_axis))], 0), which_axis, 0, 0),
+    axis=0,
+)
 
 
 def normalize(values_in, gain):
@@ -136,7 +140,7 @@
         final_rows = normalize(hidden, final_gain).astype(jnp.bfloat16)
         pool_local = all_pools[step].reshape(total_batch * width) - first_id
         raw_logits = lax.dot_general(
-            lax.all_gather(final_rows, "batch", axis=0, tiled=True),
+            make_slabs(final_rows, "batch"),
             table,
             (((1,), (1,)), ((), ())),
             preferred_element_type=jnp.float32,

time: 361 us -> 406 us (1.12)
  blocking collectives: 92.9 us -> 178 us
  waiting for transfers between devices: 180 us -> 134 us
  starting transfers between devices: 0.42 us -> 6.25 us
    all_to_all x0 -> x2, blocking collectives: none -> 65.1 us  [lax.all_to_all(jnp.stack([x0 for _ in range(lax.axis_size(which_axis))],...]
    all_gather x3 -> x0, waiting for transfers between devices: 44.7 us -> none  [per_device(): lax.all_gather(final_rows, 'batch', axis=0, tiled=True)]
    all_gather x1, blocking collectives: 14.2 us -> 34.3 us  [per_device(): lax.all_gather(pool_ids, 'batch', axis=1, tiled=True)]
    all_to_all x0 -> x1, starting transfers between devices: none -> 5.95 us  [lax.all_to_all(jnp.stack([x0 for _ in range(lax.axis_size(which_axis))],...]
  transfers between devices with their start and end apart: 6 -> 4, of which waited for: 6 -> 3; matrix products, arithmetic and copies ran while one was open for 4% -> 4% of each run, Pallas kernels for 0% -> 0%
where the time goes in v1:
time: 406 us; the launch traced here: 405 us
  blocking collectives  178 us (44%)
  waiting for transfers between devices  134 us (33%)
  local copies, waits for them, and re-layouts  31.3 us (8%)
  matrix products  24.6 us (6%)
  other arithmetic  15.9 us (4%)
  between operations  14.7 us (4%)
  starting transfers between devices  6.25 us (2%)
    all_to_all x2, blocking collectives, lax.all_to_all(jnp.stack([x0 for _ in range(lax.axis_size(which_axis))],...  65.1 us
    psum x1, waiting for transfers between devices, per_device(): whole_branch = lax.psum(branch, 'vocab')  50.6 us
    psum x1, waiting for transfers between devices, per_device(): embedded_all = lax.psum(column_rows, 'vocab').astype(jnp.float32)  47.6 us
    pmax x1, blocking collectives, per_device(): tops_joint = lax.pmax(largest, ('batch', 'vocab'))  43.5 us
    reduce_scatter x1, waiting for transfers between devices, per_device(): lax.psum_scatter(lookup_terms.astype(jnp.bfloat16), 'batch', scatter_dime...  36.1 us
    all_gather x1, blocking collectives, per_device(): lax.all_gather(pool_ids, 'batch', axis=1, tiled=True)  34.3 us
    gather x2, local copies, waits for them, and re-layouts, per_device(): looked_up = jnp.take(table, jnp.clip(ordered, 0, vocab_rows - 1), axis=0)  19.4 us
    all_gather x1, blocking collectives, per_device(): lax.all_gather(window_ids, 'batch', axis=1, tiled=True)  14.3 us
  transfers between devices with their start and end apart: 4, of which 3 were waited for; matrix products, arithmetic and copies ran while one was open for 4% of the time, Pallas kernels for 0%

profile of v1, /device:TPU:10, one launch (start us, length us, event | category | flops | bytes accessed | tf_op | source)
XLA Modules:
  0.0 405.5 jit_solution(11319681605078466096)
XLA Ops:
  8.1 14.3 %all_gather.6 = s32[3,16,8]{2,0,1:T(4,128)S(1)} all-gather(s32[3,2,8]{2,0,1:T(4,128)S(1)} %copy.76), channel_id=1, replica_groups=mesh['batch'=8,'vocab'=4] {'batch'}, dimensions={1}, use_global_device_ids=true | all-gather | bytes 1728 | tf_op jit(solution)/shard_map/all_gather | solution.py:79
  22.8 12.2 %gather_fusion = bf16[384,4608]{1,0:T(8,128)(2,1)} fusion(bf16[512,4608]{1,0:T(8,128)(2,1)} %param.20, s32[1024]{0:T(1024)S(1)} %pad_clamp_fusion), kind=kCustom, calls=%fused_computation | custom fusion | bytes 7079424 | tf_op jit(solution)/shard_map/jit(_take)/gather | solution.py:86
  35.0 7.3 %reshape.736 = bf16[16,8,3,4608]{3,2,1,0:T(4,128)(2,1)} reshape(bf16[384,4608]{1,0:T(8,128)(2,1)} %gather_fusion) | data formatting | bytes 7077888 | tf_op jit(solution)/shard_map/jit(_take)/gather | solution.py:86
  42.4 6.3 %select_convert_fusion = bf16[16,8,3,4608]{3,1,2,0:T(8,128)(2,1)} fusion(bf16[16,8,3,4608]{3,2,1,0:T(4,128)(2,1)} %reshape.736, pred[16,8,3]{1,2,0:T(4,128)(4,1)S(1)} %copy.79, pred[16,8,3]{1,2,0:T(4,128)(4,1)S(1)} %copy.78), kind=kLoop, calls=%fused_computation.1 | loop fusion | flops 7077888 | bytes 7078656 | tf_op jit(solution)/shard_map/convert_element_type | solution.py:89
  48.8 4.3 %copy.102 = bf16[256,4608]{1,0:T(8,128)(2,1)} copy(bf16[256,4608]{0,1:T(8,128)(2,1)} %bitcast.319) | data formatting | bytes 4718592 | tf_op jit(solution)/shard_map/dot_general | solution.py:112
  53.7 36.1 %reduce-scatter.2.cloned.1.call-done = bf16[2,8,3,4608]{3,1,2,0:T(8,128)(2,1)} async-done(((bf16[16,8,3,4608]{3,1,2,0:T(8,128)(2,1)}), bf16[2,8,3,4608]{3,1,2,0:T(8,128)(2,1)}) %reduce-scatter.2.cloned.1.call-update) | async-done | bytes 442384 | tf_op jit(solution)/shard_map/reduce_scatter | solution.py:88
  89.8 1.8 copy.82
  92.1 47.6 %all-reduce.13.cloned.1.call-done = bf16[2,8,3,4608]{3,1,0,2:T(8,128)(2,1)} async-done(((bf16[2,8,3,4608]{3,1,0,2:T(8,128)(2,1)}), bf16[2,8,3,4608]{3,1,0,2:T(8,128)(2,1)}) %all-reduce.13.cloned.1.call-update) | async-done | bytes 442384 | tf_op jit(solution)/shard_map/psum | solution.py:91
  141.1 1.6 fusion.45
  142.7 1.7 fusion.48
  151.1 1.2 fusion.70
  152.4 1.2 fusion.69
  153.6 50.6 %all-reduce.15.cloned.1.call-done = (f32[16,4608]{1,0:T(8,128)}, f32[16,4608]{1,0:T(8,128)}, f32[16,4608]{1,0:T(8,128)}) async-done(((f32[16,4608]{1,0:T(8,128)}, f32[16,4608]{1,0:T(8,128)}, f32[16,4608]{1,0:T(8,128)}), (f32[16,4608]{1,0:T(8,128)}, f32[16,4608]{1,0:T(8,128)}, f32[16,4608]{1,0:T(8,128)})) %all-reduce.15.cloned.1.call-update) | async-done | bytes 884752 | tf_op jit(solution)/shard_map/psum | solution.py:138
  207.6 1.5 multiply_reduce_fusion.4
  209.6 32.6 %all_to_all.15 = bf16[8,16,4608]{2,1,0:T(8,128)(2,1)} all-to-all(bf16[8,16,4608]{2,1,0:T(8,128)(2,1)S(1)} %stack.12), channel_id=1, replica_groups=mesh['batch'=8,'vocab'=4] {'batch'}, dimensions={0} | all-to-all | bytes 2359296 | tf_op jit(solution)/shard_map/all_to_all | solution.py:12
  242.3 32.5 %all_to_all.16 = bf16[8,16,4608]{2,1,0:T(8,128)(2,1)} all-to-all(bf16[8,16,4608]{2,1,0:T(8,128)(2,1)S(1)} %stack.13), channel_id=1, replica_groups=mesh['batch'=8,'vocab'=4] {'batch'}, dimensions={0} | all-to-all | bytes 2359296 | tf_op jit(solution)/shard_map/all_to_all | solution.py:12
  275.9 5.9 %all-to-all-start.2 = ((bf16[8,16,4608]{2,1,0:T(8,128)(2,1)}), bf16[8,16,4608]{2,1,0:T(8,128)(2,1)}, u32[]{:S(2)}, u32[]{:S(2)}) async-start(bf16[8,16,4608]{2,1,0:T(8,128)(2,1)} %stack.14), calls=%async_computation.3 | async-start | bytes 2359296 | tf_op jit(solution)/shard_map/all_to_all | solution.py:12
  281.9 34.3 %all_gather.7 = s32[3,16,8]{2,0,1:T(4,128)S(1)} all-gather(s32[3,2,8]{2,0,1:T(4,128)S(1)} %copy.92), channel_id=1, replica_groups=mesh['batch'=8,'vocab'=4] {'batch'}, dimensions={1}, use_global_device_ids=true | all-gather | bytes 1728 | tf_op jit(solution)/shard_map/all_gather | solution.py:80
  317.8 4.6 %select_reduce_fusion.2 = (f32[128]{0:T(128)S(1)}, f32[128]{0:T(128)S(1)}, f32[128]{0:T(128)S(1)}) fusion(s32[128]{0:T(128)S(1)} %sub.79, bf16[128,4608]{1,0:T(8,128)(2,1)} %bitcast.318, bf16[512,4608]{1,0:T(8,128)(2,1)} %param.20), kind=kOutput, calls=%fused_computation.103 | convolution fusion | flops 604438144 | bytes 5900288 | tf_op jit(solution)/shard_map/dot_general | solution.py:142
  322.4 4.1 %select_reduce_fusion.1 = (f32[128]{0:T(128)S(1)}, f32[128]{0:T(128)S(1)}, f32[128]{0:T(128)S(1)}) fusion(s32[128]{0:T(128)S(1)} %sub.82, bf16[128,4608]{1,0:T(8,128)(2,1)S(1)} %bitcast.317, bf16[512,4608]{1,0:T(8,128)(2,1)} %param.20), kind=kOutput, calls=%fused_computation.101 | convolution fusion | flops 604438144 | bytes 5900288 | tf_op jit(solution)/shard_map/dot_general | solution.py:142
  326.5 4.5 %select_reduce_fusion = (f32[128]{0:T(128)S(1)}, f32[128]{0:T(128)S(1)}, f32[128]{0:T(128)S(1)}) fusion(s32[128]{0:T(128)S(1)} %sub.85, bf16[128,4608]{1,0:T(8,128)(2,1)} %bitcast.90, bf16[512,4608]{1,0:T(8,128)(2,1)} %param.20), kind=kOutput, calls=%fused_computation.99 | convolution fusion | flops 604438144 | bytes 5900288 | tf_op jit(solution)/shard_map/dot_general | solution.py:142
  331.0 13.3 %all-reduce.7 = (f32[128]{0:T(128)S(1)}, f32[128]{0:T(128)S(1)}, f32[128]{0:T(128)S(1)}, f32[128]{0:T(128)S(1)}, f32[128]{0:T(128)S(1)}, /*index=5*/f32[128]{0:T(128)S(1)}) all-reduce(f32[128]{0:T(128)S(1)} %get-tuple-element.17, f32[128]{0:T(128)S(1)} %get-tuple-element.14, ...), channel_id=5, replica_groups=mesh['batch'=8,'vocab'=4] {'batch'}, use_global_device_ids=true, to_apply=%region_24.25.clone | all-reduce | flops 768 | bytes 6144
  344.8 7.9 %all-reduce.8 = (f32[16]{0:T(128)S(1)}, f32[16]{0:T(128)S(1)}, f32[16]{0:T(128)S(1)}, f32[16]{0:T(128)S(1)}, f32[16]{0:T(128)S(1)}, /*index=5*/f32[16]{0:T(128)S(1)}) all-reduce(f32[16]{0:T(128)S(1)} %dynamic-slice.5, f32[16]{0:T(128)S(1)} %dynamic-slice.3, f32[16]{0:T(128)S(1)} %dynamic-slice.1, ...), channel_id=1, replica_groups=mesh['batch'=8,'vocab'=4] {'vocab'}, use_global_device_ids=true, to_apply=%region_25.26 | all-reduce | flops 96 | bytes 768 | tf_op jit(solution)/shard_map/psum | solution.py:159
  353.0 43.5 %all-reduce.6 = (f32[128]{0:T(128)S(1)}, f32[128]{0:T(128)S(1)}, f32[128]{0:T(128)S(1)}) all-reduce(f32[128]{0:T(128)S(1)} %get-tuple-element.16, f32[128]{0:T(128)S(1)} %get-tuple-element.13, f32[128]{0:T(128)S(1)} %get-tuple-element.10), channel_id=1, replica_groups=mesh['batch'=8,'vocab'=4] {'batch','vocab'}, use_global_device_ids=true, to_apply=%region_31.32 | all-reduce | flops 384 | bytes 3072 | tf_op jit(solution)/shard_map/pmax | solution.py:160
  (131 shorter events, 19.8 us)
Async XLA Ops:
  7.2 142.7 %copy-start = (bf16[256,4608]{1,0:T(8,128)(2,1)S(1)}, bf16[256,4608]{1,0:T(8,128)(2,1)}, u32[]{:S(2)}) copy-start(bf16[256,4608]{1,0:T(8,128)(2,1)} %param.27) | copy-start | bytes 7077892
  7.2 82.6 %reduce-scatter.2.cloned.1.call-start = ((), (), s32[]{:S(2)}) async-start(), calls=%async_computation.4 | async-start | bytes 3981312 | tf_op jit(solution)/shard_map/reduce_scatter | solution.py:88
  48.7 90.9 %all-reduce.13.cloned.1.call-start = ((), (), s32[]{:S(2)}) async-start(), calls=%async_computation.5 | async-start | bytes 884736 | tf_op jit(solution)/shard_map/psum | solution.py:91
  48.8 4.4 %copy-start.15 = (s32[2]{0:T(128)S(1)}, s32[2]{0:T(128)}, u32[]{:S(2)}) copy-start(s32[2]{0:T(128)} %param.19) | copy-start | bytes 28
  48.8 4.5 %copy-start.13 = (s32[2,2]{1,0:T(2,128)S(1)}, s32[2,2]{1,0:T(2,128)}, u32[]{:S(2)}) copy-start(s32[2,2]{1,0:T(2,128)} %param.17) | copy-start | bytes 52
  48.8 4.5 %copy-start.14 = (s32[2,2]{1,0:T(2,128)S(1)}, s32[2,2]{1,0:T(2,128)}, u32[]{:S(2)}) copy-start(s32[2,2]{1,0:T(2,128)} %param.18) | copy-start | bytes 52
  53.2 87.9 %copy-start.5 = (f32[4608]{0:T(1024)S(1)}, f32[4608]{0:T(1024)}, u32[]{:S(2)}) copy-start(f32[4608]{0:T(1024)} %param.21) | copy-start | bytes 55300
  91.6 112.6 %all-reduce.15.cloned.1.call-start = ((), (), s32[]{:S(2)}) async-start(), calls=%async_computation.6 | async-start | bytes 1769472 | tf_op jit(solution)/shard_map/psum | solution.py:138
  139.7 4.7 %copy-start.3 = (bf16[4608,128]{1,0:T(8,128)(2,1)S(1)}, bf16[4608,128]{1,0:T(8,128)(2,1)}, u32[]{:S(2)}) copy-start(bf16[4608,128]{1,0:T(8,128)(2,1)} %param.26) | copy-start | bytes 3538948
  142.6 2.4 copy-start.2
  144.7 1.7 copy-start.1
  147.1 1.7 copy-start.16
  147.8 2.1 copy-start.9
  152.4 55.3 %copy-start.10 = (f32[4608]{0:T(1024)S(1)}, f32[4608]{0:T(1024)}, u32[]{:S(2)}) copy-start(f32[4608]{0:T(1024)} %param.22) | copy-start | bytes 55300
  153.6 55.6 %copy-start.11 = (f32[4608]{0:T(1024)S(1)}, f32[4608]{0:T(1024)}, u32[]{:S(2)}) copy-start(f32[4608]{0:T(1024)} %param.23) | copy-start | bytes 55300
  204.2 5.0 %copy-start.6 = (f32[16,4608]{1,0:T(8,128)S(1)}, f32[16,4608]{1,0:T(8,128)}, u32[]{:S(2)}) copy-start(f32[16,4608]{1,0:T(8,128)} %get-tuple-element.36) | copy-start | bytes 884740
  204.2 5.0 %copy-start.7 = (f32[16,4608]{1,0:T(8,128)S(1)}, f32[16,4608]{1,0:T(8,128)}, u32[]{:S(2)}) copy-start(f32[16,4608]{1,0:T(8,128)} %get-tuple-element.37) | copy-start | bytes 884740
  204.2 5.0 %copy-start.8 = (f32[16,4608]{1,0:T(8,128)S(1)}, f32[16,4608]{1,0:T(8,128)}, u32[]{:S(2)}) copy-start(f32[16,4608]{1,0:T(8,128)} %get-tuple-element.38) | copy-start | bytes 884740
  274.8 7.1 %copy-start.12 = (s32[3,2,8]{2,1,0:T(2,128)S(1)}, s32[3,2,8]{2,1,0:T(2,128)}, u32[]{:S(2)}) copy-start(s32[3,2,8]{2,1,0:T(2,128)} %param.16) | copy-start | bytes 580
  274.8 41.7 %copy-start.17 = (u32[32]{0:T(128)S(1)}, u32[32]{0:T(128)}, u32[]{:S(2)}) copy-start(u32[32]{0:T(128)} %constant.94) | copy-start | bytes 388
  275.9 50.6 %all-to-all-start.2 = ((bf16[8,16,4608]{2,1,0:T(8,128)(2,1)}), bf16[8,16,4608]{2,1,0:T(8,128)(2,1)}, u32[]{:S(2)}, u32[]{:S(2)}) async-start(bf16[8,16,4608]{2,1,0:T(8,128)(2,1)} %stack.14), calls=%async_computation.3 | async-start | bytes 2359296 | tf_op jit(solution)/shard_map/all_to_all | solution.py:12
  317.8 4.6 %copy-start.4 = (bf16[8,16,4608]{2,1,0:T(8,128)(2,1)S(1)}, bf16[8,16,4608]{2,1,0:T(8,128)(2,1)}, u32[]{:S(2)}) copy-start(bf16[8,16,4608]{2,1,0:T(8,128)(2,1)} %all_to_all.16) | copy-start | bytes 3538948
Sparse Core Ops, SparseCore 0:
  48.9 40.8 reduce-scatter.1
  92.8 46.8 all-reduce.12
  153.7 50.3 all-reduce.14
